TPU v7x, 128 devices: a whole 4x4x4 slice. The times are simulated.
128 devices in a mesh: ba: 16 (over y_lo, z, core), ha: 8 (over y_hi, x).
Axes of the slice: x: 4, y: 4 (y_hi: 2, y_lo: 2; y = y_hi * 2 + y_lo), z: 4, core: 2. Of those that a mesh axis runs over, the one named last changes fastest.
Arguments:
- queries: bfloat16 [4096, 64, 576], P('ba', 'ha'), may hold values from -6 to 6
- out_grad: bfloat16 [4096, 64, 512], P('ba', 'ha'), may hold values from -1.1953125 to 1.1953125
- out_saved: bfloat16 [4096, 64, 512], P('ba', 'ha'), may hold values from -3 to 3
- logsumexp: float32 [4096, 64], P('ba', 'ha'), may hold values from 7 to 9
- parents: int32 [4096], P('ba'), may hold values from 0 to 1023, as said below
- latents: bfloat16 [1024, 576], P(('ba', 'ha')), may hold values from -6 to 6
- hidden: bfloat16 [1024, 7168], P('ba', 'ha'), may hold values from -6 to 6
- latent_weight: bfloat16 [576, 7168], P(None, 'ha'), may hold values from -0.0625 to 0.0625
Outputs:
- query_grad: bfloat16 [4096, 64, 576], P('ba', 'ha')
- weight_grad: bfloat16 [576, 7168], P('ba', 'ha')
- input_grad: bfloat16 [1024, 7168], P('ba', 'ha')
Inputs may be any that keep to these rules, and one draw needn't show every extreme that they name: `parents`: the 32 tokens of each aligned block of 32 share one value; some token has 0 and some has 1023.
All inputs are finite; a program needn't handle non-finite values.
Results may differ from a plain program's by a relative error of at most 0.0067.
Values may be sent and summed in bfloat16 or wider, within the bound.
A program may use at most 64 MiB of HBM per device.

v0:
```python
import jax
import jax.numpy as jnp
from jax import lax
from jax.sharding import PartitionSpec as P

RANK = 512
ROPE = 64
softmax_scale = 192.0 ** (-0.5)


def cut_along(shard, dim, peers):
    before, after = (shard.shape[:dim], shard.shape[dim + 1 :])
    return jnp.moveaxis(shard.reshape(*before, peers, -1, *after), dim, 0)


def sent_and_summed(shard, axis, dim):
    peers = lax.axis_size(axis)
    pieces = lax.all_to_all(cut_along(shard, dim, peers), axis, 0, 0, tiled=True)
    return jnp.sum(pieces, axis=0)


def from_everyone(shard, axis):
    peers = lax.axis_size(axis)
    return lax.all_to_all(
        jnp.broadcast_to(shard[None], (peers, *shard.shape)), axis, 0, 0, tiled=True
    )


def over_copies(shard, axis):
    return from_everyone(shard, axis).sum(axis=0)


def tile_terms(query_rows, grad_rows, lse_rows, deltas, limits, key_block, offset):
    key_count = key_block.shape[0]
    key_index = offset + jnp.arange(key_count, dtype=jnp.int32)
    scores = (
        jnp.einsum("qd,kd->qk", query_rows, key_block, preferred_element_type=jnp.float32)
        * softmax_scale
    )
    visible = key_index[None, :] <= limits[:, None]
    weights = jnp.where(visible, jnp.exp(scores - lse_rows[:, None]), jnp.float32(0.0))
    grad_prob = jnp.einsum(
        "qd,kd->qk", grad_rows, key_block[:, :RANK], preferred_element_type=jnp.float32
    )
    grad_score = (weights * (grad_prob - deltas[:, None])).astype(jnp.bfloat16)
    query_part = jnp.einsum("qk,kd->qd", grad_score, key_block, preferred_element_type=jnp.float32)
    value_part = jnp.einsum(
        "qk,qd->kd", weights.astype(jnp.bfloat16), grad_rows, preferred_element_type=jnp.float32
    )
    key_grad = softmax_scale * jnp.einsum(
        "qk,qd->kd", grad_score, query_rows, preferred_element_type=jnp.float32
    )
    key_grad = key_grad + jnp.pad(value_part, ((0, 0), (0, ROPE)))
    return (query_part, key_grad)


def on_device(queries, out_grad, out_saved, logsumexp, parents, latents, hidden, latent_weight):
    tokens_here, heads_here, full_width = queries.shape
    row_total = tokens_here * heads_here
    query_rows = queries.reshape(row_total, full_width)
    grad_rows = out_grad.reshape(row_total, RANK)
    saved_rows = out_saved.reshape(row_total, RANK)
    lse_rows = logsumexp.reshape(row_total)
    limits = jnp.repeat(parents, heads_here)
    deltas = jnp.sum(saved_rows.astype(jnp.float32) * grad_rows.astype(jnp.float32), axis=1)
    all_keys = lax.all_gather(latents, ("ba", "ha"), axis=0, tiled=True)
    prefix_total = all_keys.shape[0]
    tile_len = min(256, prefix_total)
    tile_count = prefix_total // tile_len
    key_tiles = all_keys.reshape(tile_count, tile_len, full_width)
    offsets = jnp.arange(tile_count, dtype=jnp.int32) * tile_len

    def tile_step(query_acc, tile_inputs):
        key_block, offset = tile_inputs
        query_part, key_grad = tile_terms(
            query_rows, grad_rows, lse_rows, deltas, limits, key_block, offset
        )
        return (query_acc + query_part, key_grad)

    query_acc, key_stack = lax.scan(
        tile_step, jnp.zeros((row_total, full_width), jnp.float32), (key_tiles, offsets)
    )
    latent_acc = key_stack.reshape(prefix_total, full_width)
    query_grad = (
        (softmax_scale * query_acc)
        .astype(jnp.bfloat16)
        .reshape(tokens_here, heads_here, full_width)
    )
    branch_part = sent_and_summed(latent_acc, "ba", 0)
    row_grads = over_copies(branch_part, "ha").astype(jnp.bfloat16)
    weight_grad = sent_and_summed(
        jnp.einsum("pl,ph->lh", row_grads, hidden, preferred_element_type=jnp.float32), "ba", 0
    ).astype(jnp.bfloat16)
    input_grad = jnp.dot(row_grads, latent_weight, preferred_element_type=jnp.float32).astype(
        jnp.bfloat16
    )
    return (query_grad, weight_grad, input_grad)


def solution(mesh):
    return jax.shard_map(
        on_device,
        mesh=mesh,
        in_specs=(
            P("ba", "ha", None),
            P("ba", "ha", None),
            P("ba", "ha", None),
            P("ba", "ha"),
            P("ba"),
            P(("ba", "ha"), None),
            P("ba", "ha"),
            P(None, "ha"),
        ),
        out_specs=(P("ba", "ha", None), P("ba", "ha"), P("ba", "ha")),
        check_vma=False,
    )
```

profile of v0, /device:TPU:97, one launch (start us, length us, event | category | flops | bytes accessed | tf_op | source)
XLA Modules:
  0.0 485.5 jit_solution(854251680802731591)
XLA Ops:
  7.9 0.8 copy.21
  8.9 2.8 multiply_reduce_fusion
  11.9 5.1 %copy.20 = bf16[256,8,576]{2,1,0:T(8,128)(2,1)} copy(bf16[256,8,576]{0,2,1:T(8,128)(2,1)} %param.10) | data formatting | bytes 4718592 | tf_op args[0]
  16.9 295.1 %all-gather.2.cloned.1.call-done = bf16[1024,576]{1,0:T(8,128)(2,1)} async-done(((bf16[8,576]{1,0:T(8,128)(2,1)}), bf16[1024,576]{1,0:T(8,128)(2,1)}) %all-gather.2.cloned.1.call-update) | async-done | bytes 1179664 | tf_op jit(solution)/shard_map/all_gather | solution.py:66
  312.0 55.1 %while.16 = (s32[]{:T(128)}, f32[2048,576]{0,1:T(8,128)}, f32[4,256,576]{1,2,0:T(8,128)}, s32[4]{0:T(128)S(1)}, bf16[4,256,576]{2,1,0:T(8,128)(2,1)}, /*index=5*...) while((s32[]{:T(128)}, f32[2048,576]{0,1:T(8,128)}, ...), condition=%wide.wide.region_2.3_spmd.clone, body=%wide.wide.region_1.2_spmd.clone.sunk | while | flops 2892529920 | bytes 73387280 | solution.py:80
  313.4 1.0 dynamic-slice_bitcast_fusion.3
  314.5 2.8 fusion.69
  317.3 1.0 fusion.71
  319.1 1.2 copy-done.3
  320.3 2.0 fusion.72
  322.3 1.4 select_add_fusion.3
  323.7 2.1 copy-done.2
  327.2 1.0 dynamic-slice_bitcast_fusion.3
  328.2 2.8 fusion.69
  331.1 1.0 fusion.71
  332.1 0.7 fusion.70
  332.8 1.2 copy-done.3
  334.1 2.0 fusion.72
  336.0 1.4 select_add_fusion.3
  337.4 2.1 copy-done.2
  341.0 1.0 dynamic-slice_bitcast_fusion.3
  342.0 2.8 fusion.69
  344.9 1.0 fusion.71
  345.9 0.7 fusion.70
  346.6 1.2 copy-done.3
  347.9 2.0 fusion.72
  349.8 1.4 select_add_fusion.3
  351.2 2.1 copy-done.2
  354.8 1.0 dynamic-slice_bitcast_fusion.3
  355.8 2.8 fusion.69
  358.7 1.0 fusion.71
  359.7 0.7 fusion.70
  360.4 1.2 copy-done.3
  361.7 2.0 fusion.72
  363.6 1.4 select_add_fusion.3
  365.0 2.1 copy-done.2
  367.1 3.2 copy.23
  370.3 37.9 %all_to_all.15 = f32[16,64,576]{2,1,0:T(8,128)} all-to-all(f32[16,64,576]{2,1,0:T(8,128)} %bitcast.77), channel_id=1, replica_groups=mesh['ba'=16,'ha'=8] {'ba'}, dimensions={0} | all-to-all | bytes 4718592 | tf_op jit(solution)/shard_map/all_to_all | solution.py:18
  408.2 1.9 reduce_sum.40
  410.2 25.9 %all_to_all.16 = f32[8,64,576]{2,1,0:T(8,128)S(1)} all-to-all(f32[8,64,576]{2,1,0:T(8,128)S(1)} %broadcast_in_dim.34), channel_id=1, replica_groups=mesh['ba'=16,'ha'=8] {'ha'}, dimensions={0} | all-to-all | bytes 2359296 | tf_op jit(solution)/shard_map/all_to_all | solution.py:24
  436.7 1.6 reshape.35
  438.2 5.8 %all-to-all-start.2 = ((f32[16,36,896]{2,1,0:T(8,128)}), f32[16,36,896]{2,1,0:T(8,128)}, u32[]{:S(2)}, u32[]{:S(2)}) async-start(f32[16,36,896]{2,1,0:T(8,128)} %reshape.35), calls=%async_computation.2 | async-start | bytes 4587520 | tf_op jit(solution)/shard_map/all_to_all | solution.py:18
  444.0 2.9 multiply_convert_fusion
  447.0 2.6 copy.22
  449.5 4.6 copy.24
  454.2 1.0 convolution_convert_fusion
  455.1 21.1 %all-to-all-done.2 = f32[16,36,896]{2,1,0:T(8,128)} async-done(((f32[16,36,896]{2,1,0:T(8,128)}), f32[16,36,896]{2,1,0:T(8,128)}, u32[]{:S(2)}, u32[]{:S(2)}) %all-to-all-start.2) | async-done | bytes 2064416 | tf_op jit(solution)/shard_map/all_to_all | solution.py:18
  476.2 2.4 reduce_sum.42
  (65 shorter events, 8.1 us)
Async XLA Ops:
  7.2 447.0 %copy-start = (bf16[576,896]{1,0:T(8,128)(2,1)S(1)}, bf16[576,896]{1,0:T(8,128)(2,1)}, u32[]{:S(2)}) copy-start(bf16[576,896]{1,0:T(8,128)(2,1)} %param.17) | copy-start | bytes 3096580
  7.2 304.8 %all-gather.2.cloned.1.call-start = ((), (), s32[]{:S(2)}) async-start(), calls=%async_computation.3 | async-start | bytes 1320960 | tf_op jit(solution)/shard_map/all_gather | solution.py:66
  8.8 8.1 %copy-start.4 = (f32[256,8]{1,0:T(8,128)}, f32[256,8]{1,0:T(8,128)S(1)}, u32[]{:S(2)}) copy-start(f32[256,8]{1,0:T(8,128)S(1)} %copy.21) | copy-start | bytes 24580
  11.8 300.2 %copy-start.1 = (bf16[256,8,512]{2,1,0:T(8,128)(2,1)S(1)}, bf16[256,8,512]{2,1,0:T(8,128)(2,1)}, u32[]{:S(2)}) copy-start(bf16[256,8,512]{2,1,0:T(8,128)(2,1)} %param.11) | copy-start | bytes 6291460
  11.8 300.2 %copy-start.6 = (s32[256]{0:T(256)S(1)}, s32[256]{0:T(256)}, u32[]{:S(2)}) copy-start(s32[256]{0:T(256)} %param.14) | copy-start | bytes 3076
  317.3 5.0 %slice-start = ((s8[4718592]{0:T(1024)(128)(4,1)}), s8[4194304]{0:T(1024)(128)(4,1)S(1)}, s32[]{:S(2)}) async-start(s8[4718592]{0:T(1024)(128)(4,1)} %bitcast.74), calls=%async_computation.4 | async-start | bytes 8388608 | tf_op jit(solution)/shard_map/while
  318.3 2.0 copy-start.3
  318.3 4.0 slice-start.1
  323.6 2.1 copy-start.2
  331.1 5.0 %slice-start = ((s8[4718592]{0:T(1024)(128)(4,1)}), s8[4194304]{0:T(1024)(128)(4,1)S(1)}, s32[]{:S(2)}) async-start(s8[4718592]{0:T(1024)(128)(4,1)} %bitcast.74), calls=%async_computation.4 | async-start | bytes 8388608 | tf_op jit(solution)/shard_map/while
  332.1 2.0 copy-start.3
  332.1 4.0 slice-start.1
  337.4 2.1 copy-start.2
  344.9 5.0 %slice-start = ((s8[4718592]{0:T(1024)(128)(4,1)}), s8[4194304]{0:T(1024)(128)(4,1)S(1)}, s32[]{:S(2)}) async-start(s8[4718592]{0:T(1024)(128)(4,1)} %bitcast.74), calls=%async_computation.4 | async-start | bytes 8388608 | tf_op jit(solution)/shard_map/while
  345.9 2.0 copy-start.3
  345.9 4.0 slice-start.1
  351.2 2.1 copy-start.2
  358.7 5.0 %slice-start = ((s8[4718592]{0:T(1024)(128)(4,1)}), s8[4194304]{0:T(1024)(128)(4,1)S(1)}, s32[]{:S(2)}) async-start(s8[4718592]{0:T(1024)(128)(4,1)} %bitcast.74), calls=%async_computation.4 | async-start | bytes 8388608 | tf_op jit(solution)/shard_map/while
  359.6 2.0 copy-start.3
  359.6 4.0 slice-start.1
  365.0 2.1 copy-start.2
  410.2 26.0 %copy-start.5 = (bf16[64,896]{1,0:T(8,128)(2,1)S(1)}, bf16[64,896]{1,0:T(8,128)(2,1)}, u32[]{:S(2)}) copy-start(bf16[64,896]{1,0:T(8,128)(2,1)} %param.16) | copy-start | bytes 344068
  438.2 38.0 %all-to-all-start.2 = ((f32[16,36,896]{2,1,0:T(8,128)}), f32[16,36,896]{2,1,0:T(8,128)}, u32[]{:S(2)}, u32[]{:S(2)}) async-start(f32[16,36,896]{2,1,0:T(8,128)} %reshape.35), calls=%async_computation.2 | async-start | bytes 4587520 | tf_op jit(solution)/shard_map/all_to_all | solution.py:18
Sparse Core Ops, SparseCore 0:
  9.7 302.2 all-gather.1
where the time goes:
time: 486 us; the launch traced here: 485 us
  waiting for transfers between devices  317 us (65%)
  blocking collectives  63.8 us (13%)
  local copies, waits for them, and re-layouts  38.8 us (8%)
  matrix products  32.9 us (7%)
  between operations  14.1 us (3%)
  other arithmetic  12.7 us (3%)
  starting transfers between devices  5.86 us (1%)
    all_gather x1, waiting for transfers between devices, on_device(): all_keys = lax.all_gather(latents, ('ba', 'ha'), axis=0, tiled=True)  295 us
    all_to_all x1, blocking collectives, sent_and_summed(): lax.all_to_all(cut_along(shard, dim, peers), axis, 0, 0, tiled=True)  37.9 us
    all_to_all x1, blocking collectives, from_everyone(): lax.all_to_all(jnp.broadcast_to(shard[None], (peers, *shard.shape)), axis...  25.9 us
    all_to_all x1, waiting for transfers between devices, sent_and_summed(): lax.all_to_all(cut_along(shard, dim, peers), axis, 0, 0, tiled=True)  21.1 us
    while x32, local copies, waits for them, and re-layouts  13.5 us
    dot_general x4, matrix products, tile_terms(): jnp.einsum('qd,kd->qk', query_rows, key_block, preferred_element_type=jnp...  11.4 us
    unnamed x13, local copies, waits for them, and re-layouts  10.5 us
  transfers between devices with their start and end apart: 2, of which 2 were waited for; matrix products, arithmetic and copies ran while one was open for 4% of the time, Pallas kernels for 0%

commit v1 on v0

--- a/solution.py
+++ b/solution.py
@@ -63,7 +63,10 @@
     lse_rows = logsumexp.reshape(row_total)
     limits = jnp.repeat(parents, heads_here)
     deltas = jnp.sum(saved_rows.astype(jnp.float32) * grad_rows.astype(jnp.float32), axis=1)
-    all_keys = lax.all_gather(latents, ("ba", "ha"), axis=0, tiled=True)
+    all_keys = jnp.concatenate(
+        lax.all_to_all(jnp.stack([latents] * lax.axis_size(("ba", "ha"))), ("ba", "ha"), 0, 0),
+        axis=0,
+    )
     prefix_total = all_keys.shape[0]
     tile_len = min(256, prefix_total)
     tile_count = prefix_total // tile_len

time: 486 us -> 197 us (0.41)
  waiting for transfers between devices: 317 us -> 32 us
  between operations: 14.1 us -> 0.77 us
  starting transfers between devices: 5.86 us -> 16.4 us
    all_gather x1 -> x0, waiting for transfers between devices: 295 us -> none  [on_device(): all_keys = lax.all_gather(latents, ('ba', 'ha'), axis=0, tiled=True)]
    all_to_all x0 -> x1, waiting for transfers between devices: none -> 10.9 us  [on_device(): lax.all_to_all(jnp.stack([latents] * lax.axis_size(('ba', 'ha'))), ('ba',...]
    all_to_all x0 -> x1, starting transfers between devices: none -> 10.5 us  [on_device(): lax.all_to_all(jnp.stack([latents] * lax.axis_size(('ba', 'ha'))), ('ba',...]
    unnamed x13 -> x15, local copies, waits for them, and re-layouts: 10.5 us -> 9.7 us
  transfers between devices with their start and end apart: 2 -> 2, of which waited for: 2 -> 2; matrix products, arithmetic and copies ran while one was open for 4% -> 9% of each run, Pallas kernels for 0% -> 0%
where the time goes in v1:
time: 197 us; the launch traced here: 196 us
  blocking collectives  61.6 us (31%)
  local copies, waits for them, and re-layouts  40.1 us (20%)
  matrix products  32.9 us (17%)
  waiting for transfers between devices  32 us (16%)
  starting transfers between devices  16.4 us (8%)
  other arithmetic  12.1 us (6%)
    all_to_all x1, blocking collectives, sent_and_summed(): lax.all_to_all(cut_along(shard, dim, peers), axis, 0, 0, tiled=True)  37.8 us
    all_to_all x1, blocking collectives, from_everyone(): lax.all_to_all(jnp.broadcast_to(shard[None], (peers, *shard.shape)), axis...  23.8 us
    all_to_all x1, waiting for transfers between devices, sent_and_summed(): lax.all_to_all(cut_along(shard, dim, peers), axis, 0, 0, tiled=True)  21.1 us
    while x32, local copies, waits for them, and re-layouts  13.5 us
    dot_general x4, matrix products, tile_terms(): jnp.einsum('qd,kd->qk', query_rows, key_block, preferred_element_type=jnp...  11.4 us
    all_to_all x1, waiting for transfers between devices, on_device(): lax.all_to_all(jnp.stack([latents] * lax.axis_size(('ba', 'ha'))), ('ba',...  10.9 us
    all_to_all x1, starting transfers between devices, on_device(): lax.all_to_all(jnp.stack([latents] * lax.axis_size(('ba', 'ha'))), ('ba',...  10.5 us
    unnamed x15, local copies, waits for them, and re-layouts  9.7 us
  transfers between devices with their start and end apart: 2, of which 2 were waited for; matrix products, arithmetic and copies ran while one was open for 9% of the time, Pallas kernels for 0%

profile of v1, /device:TPU:97, one launch (start us, length us, event | category | flops | bytes accessed | tf_op | source)
XLA Modules:
  0.0 196.2 jit_solution(615700576185569855)
XLA Ops:
  0.7 2.1 %stack.2 = bf16[128,8,576]{2,1,0:T(8,128)(2,1)} broadcast(bf16[8,576]{1,0:T(8,128)(2,1)} %param.15), dimensions={1,2} | broadcast | bytes 1188864 | tf_op jit(solution)/shard_map/stack | solution.py:67
  2.8 10.5 %all-to-all-start = ((bf16[128,8,576]{2,1,0:T(8,128)(2,1)}), bf16[128,8,576]{2,1,0:T(8,128)(2,1)}, u32[]{:S(2)}, u32[]{:S(2)}) async-start(bf16[128,8,576]{2,1,0:T(8,128)(2,1)} %stack.2), calls=%async_computation | async-start | bytes 2621440 | tf_op jit(solution)/shard_map/all_to_all | solution.py:67
  13.6 2.2 %multiply_reduce_fusion = f32[256,8]{1,0:T(8,128)S(1)} fusion(bf16[256,8,512]{2,1,0:T(8,128)(2,1)S(1)} %copy-done.1, bf16[256,8,512]{2,1,0:T(8,128)(2,1)} %param.12), kind=kLoop, calls=%fused_computation.21 | loop fusion | flops 4192256 | bytes 4202496 | tf_op jit(solution)/shard_map/reduce_sum | solution.py:65
  15.9 4.9 %copy.20 = bf16[256,8,576]{2,1,0:T(8,128)(2,1)} copy(bf16[256,8,576]{0,2,1:T(8,128)(2,1)} %param.10) | data formatting | bytes 4718592 | tf_op args[0]
  20.9 10.9 %all-to-all-done = bf16[128,8,576]{2,1,0:T(8,128)(2,1)} async-done(((bf16[128,8,576]{2,1,0:T(8,128)(2,1)}), bf16[128,8,576]{2,1,0:T(8,128)(2,1)}, u32[]{:S(2)}, u32[]{:S(2)}) %all-to-all-start) | async-done | bytes 1179680 | tf_op jit(solution)/shard_map/all_to_all | solution.py:67
  31.7 55.1 %while.16 = (s32[]{:T(128)}, f32[2048,576]{0,1:T(8,128)}, f32[4,256,576]{1,2,0:T(8,128)}, s32[4]{0:T(128)S(1)}, bf16[4,256,576]{2,1,0:T(8,128)(2,1)}, /*index=5*...) while((s32[]{:T(128)}, f32[2048,576]{0,1:T(8,128)}, ...), condition=%wide.wide.region_2.3_spmd.clone, body=%wide.wide.region_1.2_spmd.clone.sunk | while | flops 2892529920 | bytes 73387280 | solution.py:83
  33.2 1.0 dynamic-slice_bitcast_fusion.3
  34.2 2.8 %fusion.69 = f32[2048,256]{0,1:T(8,128)S(1)} fusion(bf16[256,576]{1,0:T(8,128)(2,1)S(1)} %dynamic-slice_bitcast_fusion.3, bf16[2048,576]{1,0:T(8,128)(2,1)} %get-tuple-element.351, f32[2048]{0:T(1024)S(1)} %get-tuple-element.356, s32[2048]{0:T(1024)S(1)} %le.46, s32[256]{0:T(256)S(1)} %iota_add_fusion.3), kind=kOutput, calls=%fused_computation.9.clone.clone.1 | convolution fusion | flops 606076928 | bytes 4768768 | tf_op jit(solution)/shard_map/while/body/eval_jaxpr/qd,kd->qk/dot_general | solution.py:37
  37.0 1.0 fusion.71
  38.0 0.8 fusion.70
  38.8 1.2 copy-done.3
  40.0 2.0 fusion.72
  42.0 1.4 select_add_fusion.3
  43.4 2.1 %copy-done.2 = f32[2048,576]{0,1:T(8,128)} copy-done((f32[2048,576]{0,1:T(8,128)}, f32[2048,576]{0,1:T(8,128)S(1)}, u32[]{:S(2)}) %copy-start.2) | copy-done | bytes 4718616 | tf_op jit(solution)/shard_map/while
  46.9 1.0 dynamic-slice_bitcast_fusion.3
  47.9 2.8 %fusion.69 = f32[2048,256]{0,1:T(8,128)S(1)} fusion(bf16[256,576]{1,0:T(8,128)(2,1)S(1)} %dynamic-slice_bitcast_fusion.3, bf16[2048,576]{1,0:T(8,128)(2,1)} %get-tuple-element.351, f32[2048]{0:T(1024)S(1)} %get-tuple-element.356, s32[2048]{0:T(1024)S(1)} %le.46, s32[256]{0:T(256)S(1)} %iota_add_fusion.3), kind=kOutput, calls=%fused_computation.9.clone.clone.1 | convolution fusion | flops 606076928 | bytes 4768768 | tf_op jit(solution)/shard_map/while/body/eval_jaxpr/qd,kd->qk/dot_general | solution.py:37
  50.8 1.0 fusion.71
  52.6 1.2 copy-done.3
  53.8 2.0 fusion.72
  55.8 1.4 select_add_fusion.3
  57.2 2.1 %copy-done.2 = f32[2048,576]{0,1:T(8,128)} copy-done((f32[2048,576]{0,1:T(8,128)}, f32[2048,576]{0,1:T(8,128)S(1)}, u32[]{:S(2)}) %copy-start.2) | copy-done | bytes 4718616 | tf_op jit(solution)/shard_map/while
  60.7 1.0 dynamic-slice_bitcast_fusion.3
  61.7 2.8 %fusion.69 = f32[2048,256]{0,1:T(8,128)S(1)} fusion(bf16[256,576]{1,0:T(8,128)(2,1)S(1)} %dynamic-slice_bitcast_fusion.3, bf16[2048,576]{1,0:T(8,128)(2,1)} %get-tuple-element.351, f32[2048]{0:T(1024)S(1)} %get-tuple-element.356, s32[2048]{0:T(1024)S(1)} %le.46, s32[256]{0:T(256)S(1)} %iota_add_fusion.3), kind=kOutput, calls=%fused_computation.9.clone.clone.1 | convolution fusion | flops 606076928 | bytes 4768768 | tf_op jit(solution)/shard_map/while/body/eval_jaxpr/qd,kd->qk/dot_general | solution.py:37
  64.6 1.0 fusion.71
  65.6 0.8 fusion.70
  66.3 1.2 copy-done.3
  67.6 2.0 fusion.72
  69.5 1.4 select_add_fusion.3
  70.9 2.1 %copy-done.2 = f32[2048,576]{0,1:T(8,128)} copy-done((f32[2048,576]{0,1:T(8,128)}, f32[2048,576]{0,1:T(8,128)S(1)}, u32[]{:S(2)}) %copy-start.2) | copy-done | bytes 4718616 | tf_op jit(solution)/shard_map/while
  74.5 1.0 dynamic-slice_bitcast_fusion.3
  75.5 2.8 %fusion.69 = f32[2048,256]{0,1:T(8,128)S(1)} fusion(bf16[256,576]{1,0:T(8,128)(2,1)S(1)} %dynamic-slice_bitcast_fusion.3, bf16[2048,576]{1,0:T(8,128)(2,1)} %get-tuple-element.351, f32[2048]{0:T(1024)S(1)} %get-tuple-element.356, s32[2048]{0:T(1024)S(1)} %le.46, s32[256]{0:T(256)S(1)} %iota_add_fusion.3), kind=kOutput, calls=%fused_computation.9.clone.clone.1 | convolution fusion | flops 606076928 | bytes 4768768 | tf_op jit(solution)/shard_map/while/body/eval_jaxpr/qd,kd->qk/dot_general | solution.py:37
  78.4 1.0 fusion.71
  80.1 1.2 copy-done.3
  81.4 2.0 fusion.72
  83.3 1.4 select_add_fusion.3
  84.7 2.1 %copy-done.2 = f32[2048,576]{0,1:T(8,128)} copy-done((f32[2048,576]{0,1:T(8,128)}, f32[2048,576]{0,1:T(8,128)S(1)}, u32[]{:S(2)}) %copy-start.2) | copy-done | bytes 4718616 | tf_op jit(solution)/shard_map/while
  86.9 3.2 %copy.23 = f32[4,256,576]{2,1,0:T(8,128)} copy(f32[4,256,576]{1,2,0:T(8,128)} %get-tuple-element.130) | data formatting | bytes 4718592 | tf_op jit(solution)/shard_map/while | solution.py:83
  90.1 37.8 %all_to_all.20 = f32[16,64,576]{2,1,0:T(8,128)} all-to-all(f32[16,64,576]{2,1,0:T(8,128)} %bitcast.77), channel_id=1, replica_groups=mesh['ba'=16,'ha'=8] {'ba'}, dimensions={0} | all-to-all | bytes 4718592 | tf_op jit(solution)/shard_map/all_to_all | solution.py:18
  127.9 1.9 reduce_sum.40
  129.9 23.8 %all_to_all.21 = f32[8,64,576]{2,1,0:T(8,128)S(1)} all-to-all(f32[8,64,576]{2,1,0:T(8,128)S(1)} %broadcast_in_dim.34), channel_id=1, replica_groups=mesh['ba'=16,'ha'=8] {'ha'}, dimensions={0} | all-to-all | bytes 2359296 | tf_op jit(solution)/shard_map/all_to_all | solution.py:24
  154.2 1.6 reshape.33
  155.8 5.8 %all-to-all-start.3 = ((f32[16,36,896]{2,1,0:T(8,128)}), f32[16,36,896]{2,1,0:T(8,128)}, u32[]{:S(2)}, u32[]{:S(2)}) async-start(f32[16,36,896]{2,1,0:T(8,128)} %reshape.33), calls=%async_computation.3 | async-start | bytes 4587520 | tf_op jit(solution)/shard_map/all_to_all | solution.py:18
  161.6 2.9 %multiply_convert_fusion = bf16[2048,576]{0,1:T(8,128)(2,1)S(1)} fusion(f32[2048,576]{0,1:T(8,128)} %get-tuple-element.129), kind=kLoop, calls=%fused_computation.20 | loop fusion | flops 2359296 | bytes 7077888 | tf_op jit(solution)/shard_map/convert_element_type | solution.py:89
  164.6 2.6 %copy.22 = bf16[2048,576]{1,0:T(8,128)(2,1)} copy(bf16[2048,576]{0,1:T(8,128)(2,1)S(1)} %multiply_convert_fusion) | data formatting | bytes 4718592 | tf_op jit(solution)/shard_map/convert_element_type | solution.py:89
  167.1 4.6 %copy.24 = bf16[256,8,576]{0,2,1:T(8,128)(2,1)} copy(bf16[256,8,576]{2,1,0:T(8,128)(2,1)} %bitcast.78) | data formatting | bytes 4718592
  171.8 1.0 convolution_convert_fusion
  172.7 21.1 %all-to-all-done.3 = f32[16,36,896]{2,1,0:T(8,128)} async-done(((f32[16,36,896]{2,1,0:T(8,128)}), f32[16,36,896]{2,1,0:T(8,128)}, u32[]{:S(2)}, u32[]{:S(2)}) %all-to-all-start.3) | async-done | bytes 2064416 | tf_op jit(solution)/shard_map/all_to_all | solution.py:18
  193.8 2.4 %reduce_sum.42 = bf16[36,896]{1,0:T(8,128)(2,1)} reduce(f32[16,36,896]{2,1,0:T(8,128)} %all-to-all-done.3, f32[]{:T(128)} %constant.39.clone.1), dimensions={0}, to_apply=%region_5.6 | reduce | flops 483840 | bytes 2128900 | tf_op jit(solution)/shard_map/reduce_sum | solution.py:19
  (67 shorter events, 8.3 us)
Async XLA Ops:
  0.6 171.1 %copy-start = (bf16[576,896]{1,0:T(8,128)(2,1)S(1)}, bf16[576,896]{1,0:T(8,128)(2,1)}, u32[]{:S(2)}) copy-start(bf16[576,896]{1,0:T(8,128)(2,1)} %param.17) | copy-start | bytes 3096580
  0.6 12.7 %copy-start.7 = (f32[256,8]{0,1:T(8,128)S(1)}, f32[256,8]{0,1:T(8,128)}, u32[]{:S(2)}) copy-start(f32[256,8]{0,1:T(8,128)} %param.13) | copy-start | bytes 24580
  0.7 12.9 %copy-start.1 = (bf16[256,8,512]{2,1,0:T(8,128)(2,1)S(1)}, bf16[256,8,512]{2,1,0:T(8,128)(2,1)}, u32[]{:S(2)}) copy-start(bf16[256,8,512]{2,1,0:T(8,128)(2,1)} %param.11) | copy-start | bytes 6291460
  2.8 28.9 %all-to-all-start = ((bf16[128,8,576]{2,1,0:T(8,128)(2,1)}), bf16[128,8,576]{2,1,0:T(8,128)(2,1)}, u32[]{:S(2)}, u32[]{:S(2)}) async-start(bf16[128,8,576]{2,1,0:T(8,128)(2,1)} %stack.2), calls=%async_computation | async-start | bytes 2621440 | tf_op jit(solution)/shard_map/all_to_all | solution.py:67
  13.5 2.5 %copy-start.4 = (f32[256,8]{1,0:T(8,128)}, f32[256,8]{1,0:T(8,128)S(1)}, u32[]{:S(2)}) copy-start(f32[256,8]{1,0:T(8,128)S(1)} %copy.21) | copy-start | bytes 24580
  15.9 15.8 %copy-start.6 = (s32[256]{0:T(256)S(1)}, s32[256]{0:T(256)}, u32[]{:S(2)}) copy-start(s32[256]{0:T(256)} %param.14) | copy-start | bytes 3076
  37.0 5.0 %slice-start = ((s8[4718592]{0:T(1024)(128)(4,1)}), s8[4194304]{0:T(1024)(128)(4,1)S(1)}, s32[]{:S(2)}) async-start(s8[4718592]{0:T(1024)(128)(4,1)} %bitcast.74), calls=%async_computation.4 | async-start | bytes 8388608 | tf_op jit(solution)/shard_map/while
  38.0 2.0 %copy-start.3 = (bf16[2048,576]{1,0:T(8,128)(2,1)S(1)}, bf16[2048,576]{1,0:T(8,128)(2,1)}, u32[]{:S(2)}) copy-start(bf16[2048,576]{1,0:T(8,128)(2,1)} %get-tuple-element.351) | copy-start | bytes 7077892 | tf_op jit(solution)/shard_map/while
  38.0 4.0 %slice-start.1 = ((s8[4718592]{0:T(1024)(128)(4,1)}), s8[524288]{0:T(1024)(128)(4,1)S(1)}, s32[]{:S(2)}) async-start(s8[4718592]{0:T(1024)(128)(4,1)} %bitcast.74), calls=%async_computation.5 | async-start | bytes 1048576 | tf_op jit(solution)/shard_map/while
  43.4 2.1 %copy-start.2 = (f32[2048,576]{0,1:T(8,128)}, f32[2048,576]{0,1:T(8,128)S(1)}, u32[]{:S(2)}) copy-start(f32[2048,576]{0,1:T(8,128)S(1)} %select_add_fusion.3) | copy-start | bytes 14155780 | tf_op jit(solution)/shard_map/while
  50.8 5.0 %slice-start = ((s8[4718592]{0:T(1024)(128)(4,1)}), s8[4194304]{0:T(1024)(128)(4,1)S(1)}, s32[]{:S(2)}) async-start(s8[4718592]{0:T(1024)(128)(4,1)} %bitcast.74), calls=%async_computation.4 | async-start | bytes 8388608 | tf_op jit(solution)/shard_map/while
  51.8 2.0 %copy-start.3 = (bf16[2048,576]{1,0:T(8,128)(2,1)S(1)}, bf16[2048,576]{1,0:T(8,128)(2,1)}, u32[]{:S(2)}) copy-start(bf16[2048,576]{1,0:T(8,128)(2,1)} %get-tuple-element.351) | copy-start | bytes 7077892 | tf_op jit(solution)/shard_map/while
  51.8 4.0 %slice-start.1 = ((s8[4718592]{0:T(1024)(128)(4,1)}), s8[524288]{0:T(1024)(128)(4,1)S(1)}, s32[]{:S(2)}) async-start(s8[4718592]{0:T(1024)(128)(4,1)} %bitcast.74), calls=%async_computation.5 | async-start | bytes 1048576 | tf_op jit(solution)/shard_map/while
  57.1 2.1 %copy-start.2 = (f32[2048,576]{0,1:T(8,128)}, f32[2048,576]{0,1:T(8,128)S(1)}, u32[]{:S(2)}) copy-start(f32[2048,576]{0,1:T(8,128)S(1)} %select_add_fusion.3) | copy-start | bytes 14155780 | tf_op jit(solution)/shard_map/while
  64.6 5.0 %slice-start = ((s8[4718592]{0:T(1024)(128)(4,1)}), s8[4194304]{0:T(1024)(128)(4,1)S(1)}, s32[]{:S(2)}) async-start(s8[4718592]{0:T(1024)(128)(4,1)} %bitcast.74), calls=%async_computation.4 | async-start | bytes 8388608 | tf_op jit(solution)/shard_map/while
  65.6 2.0 %copy-start.3 = (bf16[2048,576]{1,0:T(8,128)(2,1)S(1)}, bf16[2048,576]{1,0:T(8,128)(2,1)}, u32[]{:S(2)}) copy-start(bf16[2048,576]{1,0:T(8,128)(2,1)} %get-tuple-element.351) | copy-start | bytes 7077892 | tf_op jit(solution)/shard_map/while
  65.6 4.0 %slice-start.1 = ((s8[4718592]{0:T(1024)(128)(4,1)}), s8[524288]{0:T(1024)(128)(4,1)S(1)}, s32[]{:S(2)}) async-start(s8[4718592]{0:T(1024)(128)(4,1)} %bitcast.74), calls=%async_computation.5 | async-start | bytes 1048576 | tf_op jit(solution)/shard_map/while
  70.9 2.1 %copy-start.2 = (f32[2048,576]{0,1:T(8,128)}, f32[2048,576]{0,1:T(8,128)S(1)}, u32[]{:S(2)}) copy-start(f32[2048,576]{0,1:T(8,128)S(1)} %select_add_fusion.3) | copy-start | bytes 14155780 | tf_op jit(solution)/shard_map/while
  78.4 5.0 %slice-start = ((s8[4718592]{0:T(1024)(128)(4,1)}), s8[4194304]{0:T(1024)(128)(4,1)S(1)}, s32[]{:S(2)}) async-start(s8[4718592]{0:T(1024)(128)(4,1)} %bitcast.74), calls=%async_computation.4 | async-start | bytes 8388608 | tf_op jit(solution)/shard_map/while
  79.4 2.0 %copy-start.3 = (bf16[2048,576]{1,0:T(8,128)(2,1)S(1)}, bf16[2048,576]{1,0:T(8,128)(2,1)}, u32[]{:S(2)}) copy-start(bf16[2048,576]{1,0:T(8,128)(2,1)} %get-tuple-element.351) | copy-start | bytes 7077892 | tf_op jit(solution)/shard_map/while
  79.4 4.0 %slice-start.1 = ((s8[4718592]{0:T(1024)(128)(4,1)}), s8[524288]{0:T(1024)(128)(4,1)S(1)}, s32[]{:S(2)}) async-start(s8[4718592]{0:T(1024)(128)(4,1)} %bitcast.74), calls=%async_computation.5 | async-start | bytes 1048576 | tf_op jit(solution)/shard_map/while
  84.7 2.1 %copy-start.2 = (f32[2048,576]{0,1:T(8,128)}, f32[2048,576]{0,1:T(8,128)S(1)}, u32[]{:S(2)}) copy-start(f32[2048,576]{0,1:T(8,128)S(1)} %select_add_fusion.3) | copy-start | bytes 14155780 | tf_op jit(solution)/shard_map/while
  129.9 23.9 %copy-start.5 = (bf16[64,896]{1,0:T(8,128)(2,1)S(1)}, bf16[64,896]{1,0:T(8,128)(2,1)}, u32[]{:S(2)}) copy-start(bf16[64,896]{1,0:T(8,128)(2,1)} %param.16) | copy-start | bytes 344068
  155.8 38.0 %all-to-all-start.3 = ((f32[16,36,896]{2,1,0:T(8,128)}), f32[16,36,896]{2,1,0:T(8,128)}, u32[]{:S(2)}, u32[]{:S(2)}) async-start(f32[16,36,896]{2,1,0:T(8,128)} %reshape.33), calls=%async_computation.3 | async-start | bytes 4587520 | tf_op jit(solution)/shard_map/all_to_all | solution.py:18
